TPU v7x, 32 devices: a whole 2x2x4 slice. The times are simulated.
32 devices in a mesh: scen: 8 (over z, y), gen: 4 (over x, core).
Axes of the slice: x: 2, y: 2, z: 4, core: 2. Of those that a mesh axis runs over, the one named last changes fastest.
Arguments:
- zone_load: float32 [128, 16, 256], P('scen'), may hold values from 0.3 to 1
- linear_cost: float32 [16, 20480], P(None, 'gen'), may hold values from -4 to 4
- cost_diag: float32 [20480], P('gen'), may hold values from 0.5 to 2
- capacity: float32 [20480], P('gen'), may hold values from 0.5 to 2
- cost_tiles: bfloat16 [80, 256, 256], P('gen'), may hold values from -0.375 to 0.375
- coupling_tiles: bfloat16 [8, 80, 256, 256], P('scen', 'gen'), may hold values from -0.375 to 0.375
- block_map: int32 [8, 80], P('scen', 'gen'), may hold values 0 or 1
- zone_index: int32 [20480], P('gen'), may hold values from 0 to 255
- step_numer: int32 [5], replicated, may hold values from 1 to 4
- step_denom: int32 [5], replicated, may hold values from 5 to 8
Outputs:
- dispatch: float32 [128, 16, 20480], P('scen', None, 'gen')
- prices: float32 [128, 16, 256], P('scen')
- plan: float32 [16, 20480], P(None, 'gen')
All inputs are finite; a program needn't handle non-finite values. No bound on the sum of `block_map` on one device may be relied on, other than what follows from the above.
Results may differ from a plain program's by a relative error of at most 0.0003.
Values sent between devices are 32-bit elements; how exact they have to be, the bound alone decides.
No kernel may reach another device: no remote copies, remote signals or barrier semaphores. Data moves between devices by JAX's collectives and lax.ppermute only.
A program may use at most 128 MiB of HBM per device.

v0:
```python
import jax
import jax.numpy as jnp
from jax import lax
from jax.sharding import PartitionSpec as P

G = 20480
ITERS = 5
penalty = 2.0
centering = 0.5
epsilon = 1e-06


def local(
    zone_load,
    linear_cost,
    cost_diag,
    capacity,
    cost_tiles,
    coupling_tiles,
    block_map,
    zone_index,
    step_numer,
    step_denom,
):
    local_scen = zone_load.shape[0]
    periods = linear_cost.shape[0]
    zone_count = zone_load.shape[2]
    local_gen = capacity.shape[0]
    local_blocks = cost_tiles.shape[0]
    tile_width = cost_tiles.shape[2]
    gen_devices = lax.axis_size("gen")
    total_scen = local_scen * lax.axis_size("scen")
    row_count = local_scen * periods
    entries = float(total_scen * periods * G)
    coupling = coupling_tiles[0]
    block_mask = block_map[0].astype(jnp.float32)
    onehot = (zone_index[:, None] == jnp.arange(zone_count, dtype=jnp.int32)[None, :]).astype(
        jnp.float32
    )
    scen_ids = lax.axis_index("scen") * local_scen + jnp.arange(local_scen, dtype=jnp.int32)
    levels = 0.2 + 0.6 * (scen_ids.astype(jnp.float32) + 0.5) / total_scen
    dispatch = jnp.broadcast_to(levels[:, None, None] * capacity, (local_scen, periods, local_gen))
    low_dual = jnp.ones((local_scen, periods, local_gen), jnp.float32)
    high_dual = jnp.ones((local_scen, periods, local_gen), jnp.float32)
    prices = jnp.zeros((local_scen, periods, zone_count), jnp.float32)
    lowest = 0.02 * capacity
    highest = 0.98 * capacity
    plan = jnp.zeros((periods, local_gen), jnp.float32)
    for iteration in range(ITERS):
        step_size = step_numer[iteration].astype(jnp.float32) / step_denom[iteration].astype(
            jnp.float32
        )
        column_sums = lax.psum(jnp.sum(dispatch, axis=0), "scen")
        plan = column_sums / total_scen
        partial_value = jnp.dot(
            dispatch.reshape(row_count, local_gen),
            onehot,
            precision=lax.Precision.HIGHEST,
            preferred_element_type=jnp.float32,
        )
        totals = lax.psum(partial_value, "gen")
        imbalance = totals.reshape(local_scen, periods, zone_count) * (zone_count / G) - zone_load
        primal_local = jnp.sum(imbalance * imbalance) / gen_devices
        rounded = dispatch.astype(jnp.bfloat16).reshape(row_count, local_blocks, tile_width)
        cross_part = jnp.einsum(
            "rki,kij->rkj", rounded, coupling, preferred_element_type=jnp.float32
        )
        own_part = jnp.einsum(
            "rki,kij->rkj", rounded, cost_tiles, preferred_element_type=jnp.float32
        )
        products = (own_part + cross_part * block_mask[None, :, None]).reshape(
            local_scen, periods, local_gen
        )
        price_terms = jnp.dot(
            prices.reshape(row_count, zone_count),
            onehot.T,
            precision=lax.Precision.HIGHEST,
            preferred_element_type=jnp.float32,
        )
        residual = (
            cost_diag * dispatch
            + products
            + linear_cost
            + penalty * (dispatch - plan)
            + price_terms.reshape(local_scen, periods, local_gen)
            - low_dual
            + high_dual
        )
        gap_local = jnp.sum(dispatch * low_dual + (capacity - dispatch) * high_dual)
        dual_local = jnp.sum(residual * residual)
        stacked = jnp.stack([gap_local, dual_local, primal_local])
        summed = lax.psum(stacked, ("scen", "gen"))
        gap_sum = summed[0]
        dual_sq = summed[1]
        primal_sq = summed[2]
        target = centering * gap_sum / (2.0 * entries)
        dual_rms = jnp.sqrt(dual_sq / entries + epsilon)
        primal_rms = jnp.sqrt(primal_sq / float(total_scen * periods * zone_count) + epsilon)
        scaling = cost_diag + penalty + low_dual / dispatch + high_dual / (capacity - dispatch)
        updated = jnp.clip(
            dispatch - step_size * residual / (scaling * (1.0 + dual_rms)), lowest, highest
        )
        low_dual = low_dual + step_size * (target / updated - low_dual)
        high_dual = high_dual + step_size * (target / (capacity - updated) - high_dual)
        prices = prices + step_size * imbalance / (1.0 + primal_rms)
        dispatch = updated
    return (dispatch, prices, plan)


def solution(mesh):
    placed = (
        P("scen", None, None),
        P(None, "gen"),
        P("gen"),
        P("gen"),
        P("gen", None, None),
        P("scen", "gen", None, None),
        P("scen", "gen"),
        P("gen"),
        P(),
        P(),
    )
    return jax.shard_map(
        local,
        mesh=mesh,
        in_specs=placed,
        out_specs=(P("scen", None, "gen"), P("scen", None, None), P(None, "gen")),
        check_vma=False,
    )
```

profile of v0, /device:TPU:0, one launch (start us, length us, event | category | flops | bytes accessed | tf_op | source)
XLA Modules:
  0.0 921.3 jit_solution(15415761440046506945)
XLA Ops:
  36.5 5.7 copy.38
  42.3 7.0 reshape.258
  52.3 71.3 %all-reduce.11.cloned.1.call-done = f32[16,5120]{1,0:T(8,128)} async-done(((f32[16,5120]{1,0:T(8,128)}), f32[16,5120]{1,0:T(8,128)}) %all-reduce.11.cloned.1.call-update) | async-done | bytes 327696 | tf_op jit(solution)/shard_map/psum | solution.py:53
  124.6 9.1 multiply_reduce_fusion.4
  135.1 40.0 %psum.107 = f32[3]{0:T(128)S(1)} all-reduce(f32[3]{0:T(128)S(1)} %pad_maximum_fusion), channel_id=1, replica_groups=mesh['scen'=8,'gen'=4] {'scen','gen'}, use_global_device_ids=true, to_apply=%region_6.0 | all-reduce | flops 3 | bytes 24 | tf_op jit(solution)/shard_map/psum | solution.py:92
  177.1 6.8 add_reduce_fusion.3
  201.9 5.7 copy.41
  207.7 7.0 reshape.262
  214.9 8.1 all-reduce.17.cloned.1.call-done
  225.3 72.3 %all-reduce.15.cloned.1.call-done = f32[16,5120]{1,0:T(8,128)} async-done(((f32[16,5120]{1,0:T(8,128)}), f32[16,5120]{1,0:T(8,128)}) %all-reduce.15.cloned.1.call-update) | async-done | bytes 327696 | tf_op jit(solution)/shard_map/psum | solution.py:53
  298.7 11.3 %multiply_reduce_fusion.3 = (f32[]{:T(128)}, f32[16,16,5120]{2,1,0:T(8,128)}) fusion(f32[16,16,5120]{2,1,0:T(8,128)} %copy-done.1, f32[5120]{0:T(1024)S(1)} %copy-done.17, f32[]{:T(128)} %bitcast.14, f32[]{:T(128)} %bitcast, s32[5120]{0:T(1024)S(1)} %copy-done.23, f32[]{:T(128)} %bitcast.13, f32[16,16,256]{2,1,0:T(8,128)S(1)} %bitcast.123, ...), kind=kOutput, calls=%fused_computation.38 | convolution fusion | flops 4054253568 | bytes 16969744 | tf_op jit(solution)/shard_map/dot_general | solution.py:74
  311.5 39.5 %psum.110 = f32[3]{0:T(128)S(1)} all-reduce(f32[3]{0:T(128)S(1)} %pad_maximum_fusion.1), channel_id=1, replica_groups=mesh['scen'=8,'gen'=4] {'scen','gen'}, use_global_device_ids=true, to_apply=%region_13.14 | all-reduce | flops 3 | bytes 24 | tf_op jit(solution)/shard_map/psum | solution.py:92
  353.0 9.8 %add_reduce_fusion.2 = (f32[]{:T(128)}, f32[16,5120]{1,0:T(8,128)}, f32[16,16,5120]{2,1,0:T(8,128)S(1)}) fusion(f32[5120]{0:T(1024)S(1)} %copy-done.17, f32[]{:T(128)} %bitcast.24, f32[]{:T(128)} %bitcast.11, f32[16,16,5120]{2,1,0:T(8,128)} %copy-done.1, f32[]{:T(128)} %bitcast.14, f32[]{:T(128)} %bitcast, f32[]{:T(128)} %bitcast.20, ...), kind=kLoop, calls=%fused_computation.33 | loop fusion | flops 43171840 | bytes 16138264 | tf_op jit(solution)/shard_map/reduce_sum | solution.py:89
  381.0 5.7 copy.44
  386.8 7.0 reshape.265
  393.9 8.0 all-reduce.21.cloned.1.call-done
  405.2 71.9 %all-reduce.19.cloned.1.call-done = f32[16,5120]{1,0:T(8,128)} async-done(((f32[16,5120]{1,0:T(8,128)}), f32[16,5120]{1,0:T(8,128)}) %all-reduce.19.cloned.1.call-update) | async-done | bytes 327696 | tf_op jit(solution)/shard_map/psum | solution.py:53
  478.1 13.2 %multiply_reduce_fusion.2 = (f32[]{:T(128)}, f32[16,16,5120]{2,1,0:T(8,128)}) fusion(f32[16,16,5120]{2,1,0:T(8,128)} %copy-done.4, f32[16,16,5120]{2,1,0:T(8,128)} %copy-done.1, f32[5120]{0:T(1024)S(1)} %copy-done.17, f32[]{:T(128)} %bitcast.24, f32[]{:T(128)} %bitcast.11, f32[]{:T(128)} %bitcast.14, f32[]{:T(128)} %bitcast, ...), kind=kOutput, calls=%fused_computation.32 | convolution fusion | flops 4065853440 | bytes 21950484 | tf_op jit(solution)/shard_map/dot_general | solution.py:74
  492.7 39.8 %psum.113 = f32[3]{0:T(128)S(1)} all-reduce(f32[3]{0:T(128)S(1)} %pad_maximum_fusion.2), channel_id=1, replica_groups=mesh['scen'=8,'gen'=4] {'scen','gen'}, use_global_device_ids=true, to_apply=%region_20.21 | all-reduce | flops 3 | bytes 24 | tf_op jit(solution)/shard_map/psum | solution.py:92
  534.5 14.1 %add_reduce_fusion.1 = (f32[]{:T(128)}, f32[16,5120]{1,0:T(8,128)}, f32[16,16,5120]{2,1,0:T(8,128)}, f32[16,16,5120]{2,1,0:T(8,128)}, f32[16,16,5120]{2,1,0:T(8,128)S(1)}) fusion(f32[5120]{0:T(1024)S(1)} %copy-done.17, f32[]{:T(128)} %bitcast.34, f32[]{:T(128)} %bitcast.21, f32[16,16,5120]{2,1,0:T(8,128)} %copy-done.4, f32[]{:T(128)} %bitcast.24, ...), kind=kLoop, calls=%fused_computation.27 | loop fusion | flops 54968320 | bytes 31866912 | tf_op jit(solution)/shard_map/reduce_sum | solution.py:89
  572.9 7.0 reshape.268
  580.0 7.8 all-reduce.25.cloned.1.call-done
  590.1 73.0 %all-reduce.23.cloned.1.call-done = f32[16,5120]{1,0:T(8,128)} async-done(((f32[16,5120]{1,0:T(8,128)}), f32[16,5120]{1,0:T(8,128)}) %all-reduce.23.cloned.1.call-update) | async-done | bytes 327696 | tf_op jit(solution)/shard_map/psum | solution.py:53
  664.2 12.4 %multiply_reduce_fusion.1 = (f32[]{:T(128)}, f32[16,16,5120]{2,1,0:T(8,128)}) fusion(f32[16,16,5120]{2,1,0:T(8,128)} %get-tuple-element.13, f32[16,16,5120]{2,1,0:T(8,128)} %get-tuple-element.12, s32[5120]{0:T(1024)S(1)} %copy-done.23, f32[16,16,256]{2,1,0:T(8,128)S(1)} %get-tuple-element.19, f32[]{:T(128)} %bitcast.33, f32[]{:T(128)} %bitcast.21, ...), kind=kOutput, calls=%fused_computation.26 | convolution fusion | flops 4042588160 | bytes 27697164 | tf_op jit(solution)/shard_map/dot_general | solution.py:74
  677.9 39.7 %psum.116 = f32[3]{0:T(128)S(1)} all-reduce(f32[3]{0:T(128)S(1)} %pad_maximum_fusion.3), channel_id=1, replica_groups=mesh['scen'=8,'gen'=4] {'scen','gen'}, use_global_device_ids=true, to_apply=%region_27.28 | all-reduce | flops 3 | bytes 24 | tf_op jit(solution)/shard_map/psum | solution.py:92
  719.6 10.6 %add_reduce_fusion = (f32[]{:T(128)}, f32[16,5120]{1,0:T(8,128)}, f32[16,16,5120]{2,1,0:T(8,128)S(1)}) fusion(f32[5120]{0:T(1024)S(1)} %copy-done.17, f32[16,16,5120]{2,1,0:T(8,128)} %get-tuple-element.12, f32[]{:T(128)} %bitcast.44, f32[]{:T(128)} %bitcast.31, f32[16,16,5120]{2,1,0:T(8,128)} %get-tuple-element.13, f32[16,16,5120]{2,1,0:T(8,128)} %copy-done.2, ...), kind=kLoop, calls=%fused_computation.21 | loop fusion | flops 32686080 | bytes 26624016 | tf_op jit(solution)/shard_map/reduce_sum | solution.py:89
  754.2 7.0 reshape.271
  761.2 8.1 all-reduce.29.cloned.1.call-done
  773.5 71.1 %all-reduce.27.cloned.1.call-done = f32[16,5120]{1,0:T(8,128)} async-done(((f32[16,5120]{1,0:T(8,128)}), f32[16,5120]{1,0:T(8,128)}) %all-reduce.27.cloned.1.call-update) | async-done | bytes 327696 | tf_op jit(solution)/shard_map/psum | solution.py:53
  845.5 14.3 %multiply_reduce_fusion = (f32[]{:T(128)}, f32[16,16,5120]{2,1,0:T(8,128)}) fusion(f32[16,16,5120]{2,1,0:T(8,128)} %get-tuple-element.13, f32[16,16,5120]{2,1,0:T(8,128)} %copy-done.3, f32[5120]{0:T(1024)S(1)} %copy-done.17, f32[16,16,5120]{2,1,0:T(8,128)} %get-tuple-element.12, f32[]{:T(128)} %bitcast.44, f32[]{:T(128)} %bitcast.31, ...), kind=kOutput, calls=%fused_computation.20 | convolution fusion | flops 4054056960 | bytes 27193356 | tf_op jit(solution)/shard_map/dot_general | solution.py:74
  861.2 39.5 %psum.119 = f32[3]{0:T(128)S(1)} all-reduce(f32[3]{0:T(128)S(1)} %pad_maximum_fusion.4), channel_id=1, replica_groups=mesh['scen'=8,'gen'=4] {'scen','gen'}, use_global_device_ids=true, to_apply=%region_34.35 | all-reduce | flops 3 | bytes 24 | tf_op jit(solution)/shard_map/psum | solution.py:92
  902.7 10.7 %maximum_minimum_fusion = f32[16,16,5120]{2,1,0:T(8,128)} fusion(f32[16,16,5120]{2,1,0:T(8,128)} %copy-done.3, f32[16,16,5120]{2,1,0:T(8,128)} %get-tuple-element.59, f32[]{:T(128)} %bitcast.50, f32[]{:T(128)} %bitcast.41, f32[5120]{0:T(1024)S(1)} %copy-done.17, f32[5120]{0:T(1024)S(1)} %broadcast_add_fusion, f32[5120]{0:T(1024)S(1)} %get-tuple-element.25, ...), kind=kLoop, calls=%fused_computation.19 | loop fusion | flops 24903680 | bytes 26296336 | tf_op jit(solution)/shard_map/jit(clip)/min | solution.py:100
  (143 shorter events, 132.3 us)
Async XLA Ops:
  7.2 24.8 %copy-start = (bf16[20,256,256]{2,1,0:T(8,128)(2,1)S(1)}, bf16[20,256,256]{2,1,0:T(8,128)(2,1)}, u32[]{:S(2)}) copy-start(bf16[20,256,256]{2,1,0:T(8,128)(2,1)} %param.14) | copy-start | bytes 7864324
  7.2 42.1 %all-reduce.13.cloned.1.call-start = ((), (), s32[]{:S(2)}) async-start(), calls=%async_computation.1 | async-start | bytes 524288 | tf_op jit(solution)/shard_map/psum | solution.py:61
  9.0 4.7 copy-start.17
  9.0 7.9 copy-start.28
  9.0 7.9 copy-start.26
  9.0 11.8 %copy-start.27 = (s32[5]{0:T(128)S(1)}, s32[5]{0:T(128)}, u32[]{:S(2)}) copy-start(s32[5]{0:T(128)} %param.19) | copy-start | bytes 64
  9.0 15.6 %copy-start.25 = (f32[5120]{0:T(1024)S(1)}, f32[5120]{0:T(1024)}, u32[]{:S(2)}) copy-start(f32[5120]{0:T(1024)} %param.12) | copy-start | bytes 61444
  13.6 110.0 %all-reduce.11.cloned.1.call-start = ((), (), s32[]{:S(2)}) async-start(), calls=%async_computation | async-start | bytes 655360 | tf_op jit(solution)/shard_map/psum | solution.py:53
  14.6 208.5 %all-reduce.17.cloned.1.call-start = ((), (), s32[]{:S(2)}) async-start(), calls=%async_computation.3 | async-start | bytes 524288 | tf_op jit(solution)/shard_map/psum | solution.py:61
  31.9 3.6 copy-start.11
  42.3 8.7 copy-start.15
  183.8 3.1 copy-start.1
  191.0 106.7 %all-reduce.15.cloned.1.call-start = ((), (), s32[]{:S(2)}) async-start(), calls=%async_computation.2 | async-start | bytes 655360 | tf_op jit(solution)/shard_map/psum | solution.py:53
  196.6 3.6 copy-start.12
  207.7 91.0 %copy-start.21 = (f32[256,256]{1,0:T(8,128)S(1)}, f32[256,256]{1,0:T(8,128)}, u32[]{:S(2)}) copy-start(f32[256,256]{1,0:T(8,128)} %copy-done.20) | copy-start | bytes 786436
  214.7 187.2 %all-reduce.21.cloned.1.call-start = ((), (), s32[]{:S(2)}) async-start(), calls=%async_computation.5 | async-start | bytes 524288 | tf_op jit(solution)/shard_map/psum | solution.py:61
  362.8 3.1 copy-start.4
  369.8 107.2 %all-reduce.19.cloned.1.call-start = ((), (), s32[]{:S(2)}) async-start(), calls=%async_computation.4 | async-start | bytes 655360 | tf_op jit(solution)/shard_map/psum | solution.py:53
  375.7 3.6 copy-start.13
  386.8 16.1 %copy-start.18 = (f32[256,256]{1,0:T(8,128)S(1)}, f32[256,256]{1,0:T(8,128)}, u32[]{:S(2)}) copy-start(f32[256,256]{1,0:T(8,128)} %all-reduce.13.cloned.1.call-done) | copy-start | bytes 786436
  393.8 194.0 %all-reduce.25.cloned.1.call-start = ((), (), s32[]{:S(2)}) async-start(), calls=%async_computation.7 | async-start | bytes 524288 | tf_op jit(solution)/shard_map/psum | solution.py:61
  548.7 3.1 copy-start.2
  555.7 107.4 %all-reduce.23.cloned.1.call-start = ((), (), s32[]{:S(2)}) async-start(), calls=%async_computation.6 | async-start | bytes 655360 | tf_op jit(solution)/shard_map/psum | solution.py:53
  561.8 3.6 copy-start.14
  572.9 91.2 %copy-start.16 = (f32[256,256]{1,0:T(8,128)S(1)}, f32[256,256]{1,0:T(8,128)}, u32[]{:S(2)}) copy-start(f32[256,256]{1,0:T(8,128)} %all-reduce.21.cloned.1.call-done) | copy-start | bytes 786436
  580.0 189.3 %all-reduce.29.cloned.1.call-start = ((), (), s32[]{:S(2)}) async-start(), calls=%async_computation.9 | async-start | bytes 524288 | tf_op jit(solution)/shard_map/psum | solution.py:61
  730.2 3.1 copy-start.3
  737.2 107.3 %all-reduce.27.cloned.1.call-start = ((), (), s32[]{:S(2)}) async-start(), calls=%async_computation.8 | async-start | bytes 655360 | tf_op jit(solution)/shard_map/psum | solution.py:53
  743.1 3.6 copy-start.10
  845.5 14.3 %copy-start.24 = (f32[16,5120]{1,0:T(8,128)}, f32[16,5120]{1,0:T(8,128)S(1)}, u32[]{:S(2)}) copy-start(f32[16,5120]{1,0:T(8,128)S(1)} %broadcast_multiply_fusion) | copy-start | bytes 983044
  902.7 10.7 %copy-start.19 = (f32[256,256]{1,0:T(8,128)S(1)}, f32[256,256]{1,0:T(8,128)}, u32[]{:S(2)}) copy-start(f32[256,256]{1,0:T(8,128)} %all-reduce.29.cloned.1.call-done) | copy-start | bytes 786436
  902.7 10.7 %copy-start.22 = (f32[16,16,256]{2,1,0:T(8,128)S(1)}, f32[16,16,256]{2,1,0:T(8,128)}, u32[]{:S(2)}) copy-start(f32[16,16,256]{2,1,0:T(8,128)} %get-tuple-element.18) | copy-start | bytes 786436
  (7 other events, 17.7 us)
Sparse Core Ops, SparseCore 0:
  13.7 35.0 all-reduce.12
  52.1 71.3 all-reduce.10
  191.1 31.9 all-reduce.16
  226.3 71.3 all-reduce.14
  370.0 31.8 all-reduce.20
  405.7 71.3 all-reduce.18
  555.8 31.9 all-reduce.24
  591.7 71.3 all-reduce.22
  737.4 31.9 all-reduce.28
  773.1 71.3 all-reduce.26
where the time goes:
time: 927 us; the launch traced here: 921 us
  waiting for transfers between devices  392 us (42%)
  blocking collectives  199 us (21%)
  local copies, waits for them, and re-layouts  108 us (12%)
  matrix products  99.4 us (11%)
  other arithmetic  87.8 us (9%)
  between operations  34.2 us (4%)
    psum x5, waiting for transfers between devices, local(): column_sums = lax.psum(jnp.sum(dispatch, axis=0), 'scen')  360 us
    psum x5, blocking collectives, local(): summed = lax.psum(stacked, ('scen', 'gen'))  199 us
    dot_general x5, matrix products, local(): jnp.dot(prices.reshape(row_count, zone_count), onehot.T, precision=lax.Pr...  60.4 us
    reduce_sum x5, other arithmetic, local(): gap_local = jnp.sum(dispatch * low_dual + (capacity - dispatch) * high_dual)  43.2 us
    reshape x5, local copies, waits for them, and re-layouts, local(): (own_part + cross_part * block_mask[None, :, None]).reshape(local_scen, p...  35 us
    psum x5, waiting for transfers between devices, local(): totals = lax.psum(partial_value, 'gen')  32 us
    add x5, local copies, waits for them, and re-layouts, local(): own_part + cross_part * block_mask[None, :, None]  28.7 us
    reshape x5, local copies, waits for them, and re-layouts, local(): dispatch.astype(jnp.bfloat16).reshape(row_count, local_blocks, tile_width)  27.8 us
  transfers between devices with their start and end apart: 10, of which 9 were waited for; matrix products, arithmetic and copies ran while one was open for 14% of the time, Pallas kernels for 0%

commit v1 on v0

--- a/solution.py
+++ b/solution.py
@@ -50,7 +50,9 @@
         step_size = step_numer[iteration].astype(jnp.float32) / step_denom[iteration].astype(
             jnp.float32
         )
-        column_sums = lax.psum(jnp.sum(dispatch, axis=0), "scen")
+        own = jnp.sum(dispatch, axis=0)
+        parts = lax.all_gather(own, "scen")
+        column_sums = jnp.sum(parts, axis=0)
         plan = column_sums / total_scen
         partial_value = jnp.dot(
             dispatch.reshape(row_count, local_gen),

time: 927 us -> 817 us (0.88)
  waiting for transfers between devices: 392 us -> 229 us
  blocking collectives: 199 us -> 231 us
  other arithmetic: 87.8 us -> 103 us
    psum x5 -> x0, waiting for transfers between devices: 360 us -> none  [local(): column_sums = lax.psum(jnp.sum(dispatch, axis=0), 'scen')]
    all_gather x0 -> x4, waiting for transfers between devices: none -> 216 us  [local(): parts = lax.all_gather(own, 'scen')]
    all_gather x0 -> x1, blocking collectives: none -> 32.7 us  [local(): parts = lax.all_gather(own, 'scen')]
    psum x5, waiting for transfers between devices: 32 us -> 10.6 us  [local(): totals = lax.psum(partial_value, 'gen')]
  transfers between devices with their start and end apart: 10 -> 9, of which waited for: 9 -> 8; matrix products, arithmetic and copies ran while one was open for 14% -> 19% of each run, Pallas kernels for 0% -> 0%
where the time goes in v1:
time: 817 us; the launch traced here: 810 us
  blocking collectives  231 us (28%)
  waiting for transfers between devices  229 us (28%)
  local copies, waits for them, and re-layouts  113 us (14%)
  other arithmetic  103 us (13%)
  matrix products  99.4 us (12%)
  between operations  33.3 us (4%)
    all_gather x4, waiting for transfers between devices, local(): parts = lax.all_gather(own, 'scen')  216 us
    psum x5, blocking collectives, local(): summed = lax.psum(stacked, ('scen', 'gen'))  198 us
    dot_general x5, matrix products, local(): jnp.dot(prices.reshape(row_count, zone_count), onehot.T, precision=lax.Pr...  60.4 us
    reduce_sum x5, other arithmetic, local(): gap_local = jnp.sum(dispatch * low_dual + (capacity - dispatch) * high_dual)  43.2 us
    reshape x5, local copies, waits for them, and re-layouts, local(): (own_part + cross_part * block_mask[None, :, None]).reshape(local_scen, p...  34.9 us
    all_gather x1, blocking collectives, local(): parts = lax.all_gather(own, 'scen')  32.7 us
    add x5, local copies, waits for them, and re-layouts, local(): own_part + cross_part * block_mask[None, :, None]  28.7 us
    reshape x5, local copies, waits for them, and re-layouts, local(): dispatch.astype(jnp.bfloat16).reshape(row_count, local_blocks, tile_width)  27.8 us
  transfers between devices with their start and end apart: 9, of which 8 were waited for; matrix products, arithmetic and copies ran while one was open for 19% of the time, Pallas kernels for 0%

profile of v1, /device:TPU:0, one launch (start us, length us, event | category | flops | bytes accessed | tf_op | source)
XLA Modules:
  0.0 810.1 jit_solution(12163853243281500481)
XLA Ops:
  18.3 32.7 %all-gather = f32[40960]{0:T(1024)S(1)} all-gather(f32[5120]{0:T(1024)S(1)} %multiply_reduce_fusion.5), channel_id=3, replica_groups=mesh['scen'=8,'gen'=4] {'scen'}, dimensions={0}, use_global_device_ids=true | all-gather | bytes 184320 | tf_op jit(solution)/shard_map/all_gather | solution.py:54
  64.7 5.7 copy.53
  70.5 6.9 reshape.268
  77.4 9.1 %multiply_reduce_fusion.4 = (f32[]{:T(128)}, f32[16,16,5120]{2,1,0:T(8,128)}) fusion(s32[5120]{0:T(1024)S(1)} %copy-done.22, f32[16,5120]{1,0:T(8,128)} %broadcast_multiply_fusion.4, f32[16,5120]{1,0:T(8,128)} %param.11, f32[16,16,5120]{2,1,0:T(8,128)} %reshape.268, f32[16,5120]{1,0:T(8,128)S(1)} %get-tuple-element.22, f32[5120]{0:T(1024)S(1)} %copy-done.24), kind=kOutput, calls=%fused_computation.44 | convolution fusion | flops 4039639040 | bytes 11509764 | tf_op jit(solution)/shard_map/dot_general | solution.py:76
  90.8 40.1 %psum.71 = f32[3]{0:T(128)S(1)} all-reduce(f32[3]{0:T(128)S(1)} %pad_maximum_fusion), channel_id=1, replica_groups=mesh['scen'=8,'gen'=4] {'scen','gen'}, use_global_device_ids=true, to_apply=%region_6.0 | all-reduce | flops 3 | bytes 24 | tf_op jit(solution)/shard_map/psum | solution.py:94
  132.9 6.8 add_reduce_fusion.3
  163.4 5.7 copy.56
  169.1 7.0 reshape.272
  181.2 54.3 %all-gather.10.cloned.1.call-done = f32[128,5120]{1,0:T(8,128)} async-done(((f32[16,5120]{1,0:T(8,128)}), f32[128,5120]{1,0:T(8,128)}) %all-gather.10.cloned.1.call-update) | async-done | bytes 2621456 | tf_op jit(solution)/shard_map/all_gather | solution.py:54
  237.4 11.4 %multiply_reduce_fusion.3 = (f32[]{:T(128)}, f32[16,16,5120]{2,1,0:T(8,128)}) fusion(f32[16,16,5120]{2,1,0:T(8,128)} %copy-done.1, f32[5120]{0:T(1024)S(1)} %copy-done.17, f32[]{:T(128)} %bitcast.15, f32[]{:T(128)} %bitcast, s32[5120]{0:T(1024)S(1)} %copy-done.22, f32[]{:T(128)} %bitcast.14, f32[16,16,256]{2,1,0:T(8,128)} %bitcast.131, ...), kind=kOutput, calls=%fused_computation.38 | convolution fusion | flops 4054253568 | bytes 16969744 | tf_op jit(solution)/shard_map/dot_general | solution.py:76
  250.1 39.4 %psum.73 = f32[3]{0:T(128)S(1)} all-reduce(f32[3]{0:T(128)S(1)} %pad_maximum_fusion.1), channel_id=1, replica_groups=mesh['scen'=8,'gen'=4] {'scen','gen'}, use_global_device_ids=true, to_apply=%region_13.14 | all-reduce | flops 3 | bytes 24 | tf_op jit(solution)/shard_map/psum | solution.py:94
  291.6 9.8 %add_reduce_fusion.2 = (f32[]{:T(128)}, f32[16,5120]{1,0:T(8,128)}, f32[16,16,5120]{2,1,0:T(8,128)S(1)}) fusion(f32[5120]{0:T(1024)S(1)} %copy-done.17, f32[]{:T(128)} %bitcast.26, f32[]{:T(128)} %bitcast.11, f32[16,16,5120]{2,1,0:T(8,128)} %copy-done.1, f32[]{:T(128)} %bitcast.15, f32[]{:T(128)} %bitcast, f32[]{:T(128)} %bitcast.21, ...), kind=kLoop, calls=%fused_computation.33 | loop fusion | flops 43171840 | bytes 16138264 | tf_op jit(solution)/shard_map/reduce_sum | solution.py:91
  314.9 5.6 reshape.274
  325.1 5.7 copy.59
  330.9 7.0 reshape.275
  343.7 53.7 %all-gather.12.cloned.1.call-done = f32[128,5120]{1,0:T(8,128)} async-done(((f32[16,5120]{1,0:T(8,128)}), f32[128,5120]{1,0:T(8,128)}) %all-gather.12.cloned.1.call-update) | async-done | bytes 2621456 | tf_op jit(solution)/shard_map/all_gather | solution.py:54
  401.0 13.2 %multiply_reduce_fusion.2 = (f32[]{:T(128)}, f32[16,16,5120]{2,1,0:T(8,128)}) fusion(f32[16,16,5120]{2,1,0:T(8,128)} %copy-done.4, f32[16,16,5120]{2,1,0:T(8,128)} %copy-done.1, f32[5120]{0:T(1024)S(1)} %copy-done.17, f32[]{:T(128)} %bitcast.26, f32[]{:T(128)} %bitcast.11, f32[]{:T(128)} %bitcast.15, f32[]{:T(128)} %bitcast, ...), kind=kOutput, calls=%fused_computation.32 | convolution fusion | flops 4065853440 | bytes 21950484 | tf_op jit(solution)/shard_map/dot_general | solution.py:76
  415.6 39.7 %psum.75 = f32[3]{0:T(128)S(1)} all-reduce(f32[3]{0:T(128)S(1)} %pad_maximum_fusion.2), channel_id=1, replica_groups=mesh['scen'=8,'gen'=4] {'scen','gen'}, use_global_device_ids=true, to_apply=%region_20.21 | all-reduce | flops 3 | bytes 24 | tf_op jit(solution)/shard_map/psum | solution.py:94
  457.2 14.1 %add_reduce_fusion.1 = (f32[]{:T(128)}, f32[16,5120]{1,0:T(8,128)}, f32[16,16,5120]{2,1,0:T(8,128)}, f32[16,16,5120]{2,1,0:T(8,128)}, f32[16,16,5120]{2,1,0:T(8,128)S(1)}) fusion(f32[5120]{0:T(1024)S(1)} %copy-done.17, f32[]{:T(128)} %bitcast.37, f32[]{:T(128)} %bitcast.22, f32[16,16,5120]{2,1,0:T(8,128)} %copy-done.4, f32[]{:T(128)} %bitcast.26, ...), kind=kLoop, calls=%fused_computation.27 | loop fusion | flops 54968320 | bytes 31866912 | tf_op jit(solution)/shard_map/reduce_sum | solution.py:91
  495.0 5.7 copy.62
  500.7 7.0 reshape.278
  512.6 54.9 %all-gather.14.cloned.1.call-done = f32[128,5120]{1,0:T(8,128)} async-done(((f32[16,5120]{1,0:T(8,128)}), f32[128,5120]{1,0:T(8,128)}) %all-gather.14.cloned.1.call-update) | async-done | bytes 2621456 | tf_op jit(solution)/shard_map/all_gather | solution.py:54
  571.1 12.4 %multiply_reduce_fusion.1 = (f32[]{:T(128)}, f32[16,16,5120]{2,1,0:T(8,128)}) fusion(f32[16,16,5120]{2,1,0:T(8,128)} %get-tuple-element.13, f32[16,16,5120]{2,1,0:T(8,128)} %get-tuple-element.12, s32[5120]{0:T(1024)S(1)} %copy-done.22, f32[16,16,256]{2,1,0:T(8,128)S(1)} %get-tuple-element.19, f32[]{:T(128)} %bitcast.36, f32[]{:T(128)} %bitcast.22, ...), kind=kOutput, calls=%fused_computation.26 | convolution fusion | flops 4042588160 | bytes 27697164 | tf_op jit(solution)/shard_map/dot_general | solution.py:76
  585.0 39.4 %psum.77 = f32[3]{0:T(128)S(1)} all-reduce(f32[3]{0:T(128)S(1)} %pad_maximum_fusion.3), channel_id=1, replica_groups=mesh['scen'=8,'gen'=4] {'scen','gen'}, use_global_device_ids=true, to_apply=%region_27.28 | all-reduce | flops 3 | bytes 24 | tf_op jit(solution)/shard_map/psum | solution.py:94
  626.4 10.6 %add_reduce_fusion = (f32[]{:T(128)}, f32[16,5120]{1,0:T(8,128)}, f32[16,16,5120]{2,1,0:T(8,128)S(1)}) fusion(f32[5120]{0:T(1024)S(1)} %copy-done.17, f32[16,16,5120]{2,1,0:T(8,128)} %get-tuple-element.12, f32[]{:T(128)} %bitcast.48, f32[]{:T(128)} %bitcast.33, f32[16,16,5120]{2,1,0:T(8,128)} %get-tuple-element.13, f32[16,16,5120]{2,1,0:T(8,128)} %copy-done.2, ...), kind=kLoop, calls=%fused_computation.21 | loop fusion | flops 32686080 | bytes 26624016 | tf_op jit(solution)/shard_map/reduce_sum | solution.py:91
  650.3 5.6 reshape.280
  660.5 5.7 copy.65
  666.2 7.0 reshape.281
  679.9 53.3 %all-gather.16.cloned.1.call-done = f32[128,5120]{1,0:T(8,128)} async-done(((f32[16,5120]{1,0:T(8,128)}), f32[128,5120]{1,0:T(8,128)}) %all-gather.16.cloned.1.call-update) | async-done | bytes 2621456 | tf_op jit(solution)/shard_map/all_gather | solution.py:54
  735.1 14.2 %multiply_reduce_fusion = (f32[]{:T(128)}, f32[16,16,5120]{2,1,0:T(8,128)}) fusion(f32[16,16,5120]{2,1,0:T(8,128)} %get-tuple-element.13, f32[16,16,5120]{2,1,0:T(8,128)} %copy-done.3, f32[5120]{0:T(1024)S(1)} %copy-done.17, f32[16,16,5120]{2,1,0:T(8,128)} %get-tuple-element.12, f32[]{:T(128)} %bitcast.48, f32[]{:T(128)} %bitcast.33, ...), kind=kOutput, calls=%fused_computation.20 | convolution fusion | flops 4054056960 | bytes 27193356 | tf_op jit(solution)/shard_map/dot_general | solution.py:76
  750.6 39.2 %psum.79 = f32[3]{0:T(128)S(1)} all-reduce(f32[3]{0:T(128)S(1)} %pad_maximum_fusion.4), channel_id=1, replica_groups=mesh['scen'=8,'gen'=4] {'scen','gen'}, use_global_device_ids=true, to_apply=%region_34.35 | all-reduce | flops 3 | bytes 24 | tf_op jit(solution)/shard_map/psum | solution.py:94
  791.9 10.7 %maximum_minimum_fusion = f32[16,16,5120]{2,1,0:T(8,128)} fusion(f32[16,16,5120]{2,1,0:T(8,128)} %copy-done.3, f32[16,16,5120]{2,1,0:T(8,128)} %get-tuple-element.59, f32[]{:T(128)} %bitcast.54, f32[]{:T(128)} %bitcast.44, f32[5120]{0:T(1024)S(1)} %copy-done.17, f32[5120]{0:T(1024)S(1)} %broadcast_add_fusion, f32[5120]{0:T(1024)S(1)} %get-tuple-element.25, ...), kind=kLoop, calls=%fused_computation.19 | loop fusion | flops 24903680 | bytes 26296336 | tf_op jit(solution)/shard_map/jit(clip)/min | solution.py:102
  (144 shorter events, 142.8 us)
Async XLA Ops:
  7.2 53.0 %copy-start = (bf16[20,256,256]{2,1,0:T(8,128)(2,1)S(1)}, bf16[20,256,256]{2,1,0:T(8,128)(2,1)}, u32[]{:S(2)}) copy-start(bf16[20,256,256]{2,1,0:T(8,128)(2,1)} %param.14) | copy-start | bytes 7864324
  7.2 2.5 copy-start.22
  7.2 79.3 %all-reduce.6.cloned.1.call-start = ((), (), s32[]{:S(2)}) async-start(), calls=%async_computation | async-start | bytes 524288 | tf_op jit(solution)/shard_map/psum | solution.py:63
  9.0 4.7 copy-start.17
  9.0 6.7 copy-start.27
  9.0 6.7 copy-start.25
  9.0 8.1 copy-start.26
  13.6 165.2 %all-reduce.8.cloned.1.call-start = ((), (), s32[]{:S(2)}) async-start(), calls=%async_computation.1 | async-start | bytes 524288 | tf_op jit(solution)/shard_map/psum | solution.py:63
  60.1 2.9 copy-start.5
  60.1 3.6 copy-start.11
  70.5 6.9 copy-start.24
  77.4 10.8 %copy-start.15 = (f32[16,16,256]{2,1,0:T(8,128)S(1)}, f32[16,16,256]{2,1,0:T(8,128)}, u32[]{:S(2)}) copy-start(f32[16,16,256]{2,1,0:T(8,128)} %param.10) | copy-start | bytes 786436
  146.0 89.5 %all-gather.10.cloned.1.call-start = ((), (), s32[]{:S(2)}) async-start(), calls=%async_computation.5 | async-start | bytes 2949120 | tf_op jit(solution)/shard_map/all_gather | solution.py:54
  146.7 193.6 %all-reduce.10.cloned.1.call-start = ((), (), s32[]{:S(2)}) async-start(), calls=%async_computation.2 | async-start | bytes 524288 | tf_op jit(solution)/shard_map/psum | solution.py:63
  158.7 2.9 copy-start.6
  158.7 3.7 copy-start.12
  307.6 89.8 %all-gather.12.cloned.1.call-start = ((), (), s32[]{:S(2)}) async-start(), calls=%async_computation.6 | async-start | bytes 2949120 | tf_op jit(solution)/shard_map/all_gather | solution.py:54
  308.2 202.1 %all-reduce.12.cloned.1.call-start = ((), (), s32[]{:S(2)}) async-start(), calls=%async_computation.3 | async-start | bytes 524288 | tf_op jit(solution)/shard_map/psum | solution.py:63
  320.5 2.9 copy-start.7
  320.5 3.7 copy-start.13
  330.9 10.5 %copy-start.18 = (f32[256,256]{1,0:T(8,128)S(1)}, f32[256,256]{1,0:T(8,128)}, u32[]{:S(2)}) copy-start(f32[256,256]{1,0:T(8,128)} %all-reduce.6.cloned.1.call-done) | copy-start | bytes 786436
  477.6 89.9 %all-gather.14.cloned.1.call-start = ((), (), s32[]{:S(2)}) async-start(), calls=%async_computation.7 | async-start | bytes 2949120 | tf_op jit(solution)/shard_map/all_gather | solution.py:54
  478.4 197.6 %all-reduce.14.cloned.1.call-start = ((), (), s32[]{:S(2)}) async-start(), calls=%async_computation.4 | async-start | bytes 524288 | tf_op jit(solution)/shard_map/psum | solution.py:63
  490.3 2.9 copy-start.8
  490.3 3.7 copy-start.14
  500.7 70.4 %copy-start.16 = (f32[256,256]{1,0:T(8,128)S(1)}, f32[256,256]{1,0:T(8,128)}, u32[]{:S(2)}) copy-start(f32[256,256]{1,0:T(8,128)} %all-reduce.10.cloned.1.call-done) | copy-start | bytes 786436
  643.2 89.9 %all-gather.16.cloned.1.call-start = ((), (), s32[]{:S(2)}) async-start(), calls=%async_computation.8 | async-start | bytes 2949120 | tf_op jit(solution)/shard_map/all_gather | solution.py:54
  655.9 2.9 copy-start.9
  655.9 3.7 copy-start.10
  735.1 14.2 %copy-start.23 = (f32[16,5120]{1,0:T(8,128)}, f32[16,5120]{1,0:T(8,128)S(1)}, u32[]{:S(2)}) copy-start(f32[16,5120]{1,0:T(8,128)S(1)} %broadcast_multiply_fusion) | copy-start | bytes 983044
  791.8 10.7 %copy-start.19 = (f32[256,256]{1,0:T(8,128)S(1)}, f32[256,256]{1,0:T(8,128)}, u32[]{:S(2)}) copy-start(f32[256,256]{1,0:T(8,128)} %all-reduce.14.cloned.1.call-done) | copy-start | bytes 786436
  791.8 10.7 %copy-start.21 = (f32[16,16,256]{2,1,0:T(8,128)S(1)}, f32[16,16,256]{2,1,0:T(8,128)}, u32[]{:S(2)}) copy-start(f32[16,16,256]{2,1,0:T(8,128)} %get-tuple-element.18) | copy-start | bytes 786436
  (5 other events, 9.9 us)
Sparse Core Ops, SparseCore 0:
  13.8 34.9 all-reduce.5
  146.1 32.6 all-reduce.7
  181.1 54.3 all-gather.9
  307.7 32.5 all-reduce.9
  342.9 54.3 all-gather.11
  477.7 32.5 all-reduce.11
  513.1 54.3 all-gather.13
  643.4 32.5 all-reduce.13
  678.7 54.3 all-gather.15
